TPU v7x, 512 devices: a whole 4x4x16 slice. The times are simulated.
512 devices in a mesh: prow: 16 (over y, z_hi, core), pcol: 32 (over x, z_lo).
Axes of the slice: x: 4, y: 4, z: 16 (z_hi: 2, z_lo: 8; z = z_hi * 8 + z_lo), core: 2. Of those that a mesh axis runs over, the one named last changes fastest.
Arguments:
- tiles: bfloat16 [16, 32, 16, 256, 256], P('prow', 'pcol'), may hold values from -6 to 6
- tile_ids: int32 [16, 32, 16], P('prow', 'pcol'), may hold values from 0 to 127, as said below
- counts: int32 [16, 32], P('prow', 'pcol'), may hold values from 1 to 16, as said below
- pivots: int32 [256], replicated, may hold values from 0 to 65535, as said below
- l_inverse: bfloat16 [256, 256], P(None, 'pcol'), may hold values from -1 to 1, as said below
- u_inverse: bfloat16 [256, 256], P('prow'), may hold values from -0.125 to 0.5, as said below
Outputs:
- factored: bfloat16 [16, 32, 16, 256, 256], P('prow', 'pcol')
Inputs may be any that keep to these rules, and one draw needn't show every extreme that they name: Live slot s of device (p, q) holds local tile row tile_ids[p, q, s] // 8 and local tile column tile_ids[p, q, s] % 8; live codes of one device are distinct, padded slots hold arbitrary codes. Let R be the tile rows I >= 1 with tile (I, 0) held and C the tile columns J >= 1 with tile (0, J) held. Tile (0, 0) is held; on each prow index R takes the last one to 3 local tile rows, on each pcol index C takes the last one to 3 local tile columns, and both most counts are reached on some index. Every tile whose row is 0 or in R and whose column is 0 or in C is held; no other held tile lies in tile row 0, a tile row of R, or tile column 0. `counts`: some device has 16 live slots. Row r of tile row 0 and row pivots[r] change places; pivots[r] is r or a row of a tile row of R, and the values that differ from their r are distinct. `l_inverse`: lower triangular with unit diagonal. `u_inverse`: upper triangular with a positive diagonal.
All inputs are finite; a program needn't handle non-finite values.
Results may differ from a plain program's by a relative error of at most 0.0056.
Values may be sent and summed in bfloat16 or wider, within the bound.
No kernel may reach another device: no remote copies, remote signals or barrier semaphores. Data moves between devices by JAX's collectives and lax.ppermute only.
A program may use at most 64 MiB of HBM per device.

v0:
```python
import jax
import jax.numpy as jnp
from jax import lax
from jax.experimental import pallas as pl
from jax.experimental.pallas import tpu as pltpu
from jax.sharding import Mesh
from jax.sharding import PartitionSpec as P

SIDE = 256
SLOTS = 16
ROWS = 16
COLS = 8
LOWER = 3
UPPER = 3
LISTED = UPPER + 1
N_ROW = 16
N_Y = 4
N_PLANE = 8
N_X = 4
N_Z = 8
CHUNK = SIDE // N_PLANE
PIECE = SIDE // N_ROW
PART = SIDE // N_X
GIVEN = LISTED * CHUNK
SENT = GIVEN + 2 * PIECE
PANEL = LOWER * PART
PROW = ("y", "zh", "core")
PCOL = ("x", "zl")
BF = jnp.bfloat16
F32 = jnp.float32

SMEM = pl.BlockSpec(memory_space=pltpu.SMEM)
VMEM = pl.BlockSpec(memory_space=pltpu.VMEM)
ANY = pl.BlockSpec(memory_space=pl.ANY)


def iota(dim, rows=SIDE):
    return lax.broadcasted_iota(jnp.int32, (rows, SIDE), dim)


def hot(mask):
    return jnp.where(mask, 1.0, 0.0).astype(BF)


def times(a, b):
    return jnp.dot(a, b, preferred_element_type=F32)


def row_of():
    return (lax.axis_index("y") * 2 + lax.axis_index("zh")) * 2 + lax.axis_index("core")


def col_of():
    return lax.axis_index("x") * N_Z + lax.axis_index("zl")


def slot_of(ids, counts, s):
    code = ids[0, 0, s]
    return code // COLS, code % COLS, s < counts[0, 0]


def listed_column(col, q):
    return (col >= COLS - UPPER) | ((col == 0) & (q == 0)), jnp.where(col == 0, UPPER, COLS - 1 - col)


def spread_rows(pivots):
    return jnp.transpose(jnp.broadcast_to(pivots, (SIDE, SIDE)))


def block_rows(block, k):
    return block[:, k * CHUNK : (k + 1) * CHUNK].reshape(SIDE, SIDE)


def give_kernel(ids, counts, pivots, tiles, out, held, here, sems):
    p, q = row_of(), col_of()
    for i in range(LOWER + 1):
        for k in range(LISTED):
            here[i, k] = 0

    def place(s):
        row, col, live = slot_of(ids, counts, s)
        takes, k = listed_column(col, q)
        top = (row == 0) & (p == 0)
        i = jnp.where(top, LOWER, ROWS - 1 - row)
        return live & takes & (top | (row >= ROWS - LOWER)), i, k

    for s in range(SLOTS):
        wanted, i, k = place(s)

        @pl.when(wanted)
        def _():
            here[i, k] = 1
            pltpu.make_async_copy(tiles.at[0, 0, s], held.at[k, i], sems.at[s]).start()

    for i in range(LOWER + 1):
        for k in range(LISTED):

            @pl.when(here[i, k] == 0)
            def _():
                held[k, i] = jnp.zeros((SIDE, SIDE), BF)

    piv = spread_rows(pivots[...])
    lane, sub = iota(1), iota(0)
    leaves = ((piv // SIDE) % N_ROW != 0) & (p == 0)
    picks = [hot(piv - SIDE * (p + N_ROW * (ROWS - 1 - i)) == lane) for i in range(LOWER)]
    picks.append(hot(jnp.where(leaves, sub, piv - SIDE * p) == lane))
    pick = jnp.concatenate(picks, axis=1)

    for s in range(SLOTS):
        wanted, i, k = place(s)

        @pl.when(wanted)
        def _():
            pltpu.make_async_copy(tiles.at[0, 0, s], held.at[k, i], sems.at[s]).wait()

    for k in range(LISTED):
        rows = times(pick, held[k].reshape((LOWER + 1) * SIDE, SIDE)).astype(BF)
        out[:, k * CHUNK : (k + 1) * CHUNK] = rows.reshape(N_PLANE, CHUNK, SIDE)


def chunk_owner(pivots):
    first = (lax.axis_index("y") * 2 + lax.axis_index("core")) * CHUNK
    sub = iota(0, CHUNK)
    owner = jnp.zeros((CHUNK, SIDE), jnp.int32)
    for r in range(CHUNK):
        owner = jnp.where(sub == r, (pivots[first + r] // SIDE) % N_ROW, owner)
    return (owner // 2) % 2 == lax.axis_index("zh"), owner // 4 * 2 + owner % 2


def cross_kernel(pivots, got, upper, out):
    near, place = chunk_owner(pivots)
    frm = iota(1, CHUNK)
    pick = hot((iota(0, CHUNK) == frm % CHUNK) & (frm // CHUNK == jnp.where(near, place, 0)))
    for k in range(LISTED):
        out[k * CHUNK : (k + 1) * CHUNK] = times(pick, block_rows(got, k)).astype(BF)
    out[GIVEN:] = upper[...]


def relay_kernel(pivots, got, theirs, upper, out):
    zh = lax.axis_index("zh")
    near, place = chunk_owner(pivots)

    def wide(v):
        v = jnp.where(v, 1, 0) if v.dtype == jnp.bool_ else v
        return jnp.broadcast_to(v[None], (N_PLANE, CHUNK, SIDE)).reshape(SIDE, SIDE)

    near, place = wide(near) == 1, wide(place)
    to, frm = iota(0), iota(1)
    mine = to // CHUNK == place
    far = jnp.logical_not(near) | (mine & (zh == 1))
    source = jnp.where(mine, 0, place)
    pick = hot((to % CHUNK == frm % CHUNK) & (frm // CHUNK == source) & jnp.logical_not(far))
    for k in range(LISTED):
        other = theirs[k * CHUNK : (k + 1) * CHUNK].astype(F32)
        other = jnp.broadcast_to(other[None], (N_PLANE, CHUNK, SIDE)).reshape(SIDE, SIDE)
        rows = jnp.where(far, other, times(pick, block_rows(got, k))).astype(BF)
        out[:, k * CHUNK : (k + 1) * CHUNK] = rows.reshape(N_PLANE, CHUNK, SIDE)
    ours, others = upper[...].astype(F32), theirs[GIVEN:].astype(F32)
    for h in range(2):
        rows = jnp.where(zh == h, ours, others).astype(BF)
        out[:, GIVEN + h * PIECE : GIVEN + (h + 1) * PIECE] = jnp.broadcast_to(
            rows[None], (N_PLANE, PIECE, SIDE)
        )


def swap_in(pivots, old, tile, first):
    match = pivots - first == iota(0)
    moved = jnp.max(jnp.where(match, 1.0, 0.0), axis=1, keepdims=True) > 0.0
    return jnp.where(moved, times(hot(match), old), tile.astype(F32)).astype(BF)


def solve_kernel(ids, counts, pivots, tiles, got, *rest):
    outs, (inverse, old, held, here, sems) = rest[:N_X], rest[N_X:]
    p, q = row_of(), col_of()

    @pl.when(q == 0)
    def _():
        for i in range(LOWER + 1):
            here[i] = 0

        def place(s):
            row, col, live = slot_of(ids, counts, s)
            top = (row == 0) & (p == 0)
            i = jnp.where(top, LOWER, ROWS - 1 - row)
            return live & (col == 0) & (top | (row >= ROWS - LOWER)), i

        for s in range(SLOTS):
            wanted, i = place(s)

            @pl.when(wanted)
            def _():
                here[i] = 1
                pltpu.make_async_copy(tiles.at[0, 0, s], held.at[i], sems.at[s]).start()

        for y in range(N_Y):
            for h in range(2):
                for c in range(2):
                    r = (4 * y + 2 * h + c) * PIECE
                    a = GIVEN + h * PIECE
                    inverse[r : r + PIECE] = got[2 * y + c, a : a + PIECE]
        piv = jnp.broadcast_to(pivots[...], (SIDE, SIDE))
        old[...] = block_rows(got, UPPER)

        for s in range(SLOTS):
            wanted, i = place(s)

            @pl.when(wanted)
            def _():
                pltpu.make_async_copy(tiles.at[0, 0, s], held.at[i], sems.at[s]).wait()

        @pl.when(here[LOWER] == 1)
        def _():
            old[...] = held[LOWER]

        for i in range(LOWER):

            @pl.when(here[i] == 1)
            def _():
                swapped = swap_in(piv, old[...], held[i], SIDE * (p + N_ROW * (ROWS - 1 - i)))
                solved = times(swapped, inverse[...]).astype(BF)
                for c in range(N_X):
                    outs[c][i * PART : (i + 1) * PART] = solved[c * PART : (c + 1) * PART]

            @pl.when(here[i] == 0)
            def _():
                for c in range(N_X):
                    outs[c][i * PART : (i + 1) * PART] = jnp.zeros((PART, SIDE), BF)


def ready_kernel(ids, counts, pivots, tiles, gave, got, l0, l1, l2, l3, out, new, old):
    lower = (l0, l1, l2, l3)
    p, q = row_of(), col_of()
    piv = jnp.broadcast_to(pivots[...], (SIDE, SIDE))
    own = (spread_rows(pivots[...]) // SIDE) % N_ROW == p
    for k in range(LISTED):
        theirs = block_rows(got, k)
        ours = block_rows(gave, k)
        old[k] = theirs
        new[k] = jnp.where(own, ours.astype(F32), theirs.astype(F32)).astype(BF)

    def top(s, carry):
        row, col, live = slot_of(ids, counts, s)
        takes, k = listed_column(col, q)

        @pl.when(live & takes & (row == 0) & (p == 0))
        def _():
            old[k] = tiles[0, 0, s]

        return carry

    lax.fori_loop(0, SLOTS, top, 0)

    def step(s, carry):
        row, col, live = slot_of(ids, counts, s)
        takes, k = listed_column(col, q)
        first = (col == 0) & (q == 0)
        is_top = live & (row == 0) & (p == 0)
        is_lower = live & first & jnp.logical_not(is_top)
        is_swap = live & takes & jnp.logical_not(first) & (row >= ROWS - LOWER)
        is_kept = live & jnp.logical_not(is_top | is_lower | is_swap)

        @pl.when(is_top & first)
        def _():
            out[s] = new[UPPER]

        @pl.when(is_lower)
        def _():
            start = pl.multiple_of(jnp.clip(ROWS - 1 - row, 0, LOWER - 1) * PART, PART)
            for c in range(N_X):
                out[s, c * PART : (c + 1) * PART] = lower[c][pl.ds(start, PART)]

        @pl.when(is_swap)
        def _():
            out[s] = swap_in(piv, old[k], tiles[0, 0, s], SIDE * (p + N_ROW * row))

        @pl.when(is_kept)
        def _():
            out[s] = tiles[0, 0, s]

        @pl.when(jnp.logical_not(live))
        def _():
            out[s] = jnp.zeros((SIDE, SIDE), BF)

        return carry

    lax.fori_loop(0, SLOTS, step, 0)


def trail_kernel(ids, counts, ready, new, panel, out, held, left, upper, sems, back):
    p = row_of()

    def place(s):
        row, col, live = slot_of(ids, counts, s)
        listed = live & (col >= COLS - UPPER)
        top = listed & (row == 0) & (p == 0)
        i = jnp.clip(ROWS - 1 - row, 0, LOWER - 1)
        k = jnp.clip(COLS - 1 - col, 0, UPPER - 1)
        return top, listed & (row >= ROWS - LOWER), i, k

    for s in range(SLOTS):
        _, trails, _, _ = place(s)

        @pl.when(trails)
        def _():
            pltpu.make_async_copy(ready.at[0, 0, s], held.at[s], sems.at[s]).start()

    j = iota(1)
    e, t = j // COLS % N_Z, j % COLS
    e = (e % 2) * 4 + e // 2 % 2 * 2 + e // 4
    mine = j // PART * PART + COLS * (e ^ lax.axis_index("zl")) + t
    pieces = panel[:, PANEL:].reshape(SIDE, SIDE)
    inverse = times(hot(mine == iota(0)), pieces).astype(BF)
    for k in range(UPPER):
        upper[k] = lax.dot_general(
            inverse, new[k], (((0,), (0,)), ((), ())), preferred_element_type=F32
        ).astype(BF)
    for i in range(LOWER):
        left[i] = panel[:, i * PART : (i + 1) * PART].reshape(SIDE, SIDE)

    for s in range(SLOTS):
        top, trails, i, k = place(s)

        @pl.when(top)
        def _():
            held[s] = upper[k]

        @pl.when(trails)
        def _():
            pltpu.make_async_copy(ready.at[0, 0, s], held.at[s], sems.at[s]).wait()
            held[s] = (held[s].astype(F32) - times(left[i], upper[k])).astype(BF)

        @pl.when(top | trails)
        def _():
            pltpu.make_async_copy(held.at[s], out.at[0, 0, s], back.at[s]).start()

    for s in range(SLOTS):
        top, trails, _, _ = place(s)

        @pl.when(top | trails)
        def _():
            pltpu.make_async_copy(held.at[s], out.at[0, 0, s], back.at[s]).wait()


def call(kernel, specs, ins, shapes, scratch=(), out_space=VMEM, aliases=None):
    shapes = [jax.ShapeDtypeStruct(o, BF) for o in shapes]
    several = len(shapes) > 1
    return pl.pallas_call(
        kernel,
        out_shape=shapes if several else shapes[0],
        in_specs=[{"s": SMEM, "v": VMEM, "a": ANY}[c] for c in specs],
        out_specs=[out_space] * len(shapes) if several else out_space,
        scratch_shapes=list(scratch),
        input_output_aliases=aliases or {},
        name=kernel.__name__,
    )(*ins)


def body(tiles, tile_ids, counts, pivots, l_inverse, u_inverse):
    x = lax.axis_index("x")
    z = lax.axis_index("zl")
    lanes = pivots[None]
    tile = (SIDE, SIDE)
    plane = ("y", "core")

    gave = call(
        give_kernel,
        "ssva",
        [tile_ids, counts, lanes, tiles],
        [(N_PLANE, GIVEN, SIDE)],
        [
            pltpu.VMEM((LISTED, LOWER + 1, SIDE, SIDE), BF),
            pltpu.SMEM((LOWER + 1, LISTED), jnp.int32),
            pltpu.SemaphoreType.DMA((SLOTS,)),
        ],
    )
    got = lax.all_to_all(gave, plane, 0, 0, tiled=True)
    crossing = call(cross_kernel, "svv", [pivots, got, u_inverse], [(GIVEN + PIECE, SIDE)])
    theirs = lax.ppermute(crossing, "zh", [(0, 1), (1, 0)])
    relayed = call(
        relay_kernel, "svvv", [pivots, got, theirs, u_inverse], [(N_PLANE, SENT, SIDE)]
    )
    have = lax.all_to_all(relayed, plane, 0, 0, tiled=True)

    parts = call(
        solve_kernel,
        "ssvav",
        [tile_ids, counts, lanes, tiles, have],
        [(PANEL, SIDE)] * N_X,
        [
            pltpu.VMEM(tile, BF),
            pltpu.VMEM(tile, BF),
            pltpu.VMEM((LOWER + 1, SIDE, SIDE), BF),
            pltpu.SMEM((LOWER + 1,), jnp.int32),
            pltpu.SemaphoreType.DMA((SLOTS,)),
        ],
    )
    *parts, pieces = lax.optimization_barrier((*parts, l_inverse.T))
    part = parts[0]
    for c in range(1, N_X):
        sent = lax.ppermute(parts[c], PCOL, [(0, c * N_Z)])
        part = jnp.where(x == c, sent, part)
    for step in (4, 2, 1):
        sent = lax.ppermute(part, "zl", [(a, a + step) for a in range(0, N_Z, 2 * step)])
        part = jnp.where(z % (2 * step) == step, sent, part)
        more = lax.ppermute(pieces, "zl", [(a, a ^ step) for a in range(N_Z)])
        pieces = jnp.concatenate([pieces, more], axis=0)
    block = jnp.concatenate([part, pieces], axis=0)
    panel = lax.all_to_all(
        jnp.broadcast_to(block[None], (N_X, SIDE, SIDE)), "x", 0, 0, tiled=True
    )

    ready, new = call(
        ready_kernel,
        "ssvvvvvvvv",
        [tile_ids, counts, lanes, tiles, gave, have, *parts],
        [(SLOTS, SIDE, SIDE), (LISTED, SIDE, SIDE)],
        [pltpu.VMEM((LISTED, SIDE, SIDE), BF)],
    )
    return call(
        trail_kernel,
        "ssavv",
        [tile_ids, counts, ready[None, None], new, panel],
        [(1, 1, SLOTS, SIDE, SIDE)],
        [
            pltpu.VMEM((SLOTS, SIDE, SIDE), BF),
            pltpu.VMEM((LOWER, SIDE, SIDE), BF),
            pltpu.VMEM((UPPER, SIDE, SIDE), BF),
            pltpu.SemaphoreType.DMA((SLOTS,)),
            pltpu.SemaphoreType.DMA((SLOTS,)),
        ],
        out_space=ANY,
        aliases={2: 0},
    )


def solution(mesh):
    torus = Mesh(mesh.devices.reshape(N_Y, 2, 2, N_X, N_Z), PROW + PCOL)
    placed = (
        P(PROW, PCOL, None, None, None),
        P(PROW, PCOL, None),
        P(PROW, PCOL),
        P(),
        P(None, PCOL),
        P(PROW, None),
    )
    return jax.shard_map(
        body,
        mesh=torus,
        in_specs=placed,
        out_specs=P(PROW, PCOL, None, None, None),
        check_vma=False,
    )
```

profile of v0, /device:TPU:2, one launch (start us, length us, event | category | flops | bytes accessed | tf_op | source)
XLA Modules:
  0.0 113.2 jit_solution(11464677553415005266)
XLA Ops:
  0.7 3.5 %give_kernel.1.gave = bf16[8,128,256]{2,1,0:T(8,128)(2,1)} custom-call(s32[1,1,16]{2,1,0:T(1,128)} %ids.7, s32[1,1]{1,0:T(1,128)S(6)} %copy.13.counts, s32[1,256]{1,0:T(1,128)} %bitcast.8, bf16[1,1,16,256,256]{4,3,2,1,0:T(8,128)(2,1)} %tiles.5), custom_call_target="tpu_custom_call" | custom-call | tf_op jit(solution)/shard_map/give_kernel/pallas_call | solution.py:347
  4.2 14.8 %all_to_all.15.got = bf16[8,128,256]{2,1,0:T(8,128)(2,1)} all-to-all(bf16[8,128,256]{2,1,0:T(8,128)(2,1)} %give_kernel.1.gave), channel_id=1, replica_groups=mesh['y'=4,'zh'=2,'core'=2,'x'=4,'zl'=8] {'y','core'}, dimensions={0} | all-to-all | bytes 1048576 | tf_op jit(solution)/shard_map/all_to_all | solution.py:376
  19.0 2.1 %cross_kernel.1 = bf16[144,256]{1,0:T(8,128)(2,1)} custom-call(s32[256]{0:T(256)} %pivots.3, bf16[8,128,256]{2,1,0:T(8,128)(2,1)} %all_to_all.15.got, bf16[16,256]{1,0:T(8,128)(2,1)} %upper.3), custom_call_target="tpu_custom_call" | custom-call | tf_op jit(solution)/shard_map/cross_kernel/pallas_call | solution.py:347
  21.1 15.7 %collective-permute-start = (bf16[144,256]{1,0:T(8,128)(2,1)}, bf16[144,256]{1,0:T(8,128)(2,1)S(1)}, u32[]{:S(2)}, u32[]{:S(2)}) collective-permute-start(bf16[144,256]{1,0:T(8,128)(2,1)} %cross_kernel.1), channel_id=1, source_target_pairs={{0,64},{64,0},{1,65},{65,1},{2,66},{66,2},{3,67},{67,3},{4,68},{68... | collective-permute-start | bytes 221192 | tf_op jit(solution)/shard_map/ppermute | solution.py:378
  36.8 4.9 %collective-permute-done.theirs = bf16[144,256]{1,0:T(8,128)(2,1)S(1)} collective-permute-done((bf16[144,256]{1,0:T(8,128)(2,1)}, bf16[144,256]{1,0:T(8,128)(2,1)S(1)}, u32[]{:S(2)}, u32[]{:S(2)}) %collective-permute-start) | collective-permute-done | bytes 73760 | tf_op jit(solution)/shard_map/ppermute | solution.py:378
  41.7 0.6 copy-done.1
  42.4 2.5 %relay_kernel.1 = bf16[8,160,256]{2,1,0:T(8,128)(2,1)} custom-call(s32[256]{0:T(256)} %pivots.3, bf16[8,128,256]{2,1,0:T(8,128)(2,1)} %all_to_all.15.got, bf16[144,256]{1,0:T(8,128)(2,1)} %copy-done.1, bf16[16,256]{1,0:T(8,128)(2,1)} %upper.3), custom_call_target="tpu_custom_call" | custom-call | tf_op jit(solution)/shard_map/relay_kernel/pallas_call | solution.py:347
  44.8 16.1 %all_to_all.16.got = bf16[8,160,256]{2,1,0:T(8,128)(2,1)} all-to-all(bf16[8,160,256]{2,1,0:T(8,128)(2,1)} %relay_kernel.1), channel_id=1, replica_groups=mesh['y'=4,'zh'=2,'core'=2,'x'=4,'zl'=8] {'y','core'}, dimensions={0} | all-to-all | bytes 1310720 | tf_op jit(solution)/shard_map/all_to_all | solution.py:382
  60.9 2.0 %solve_kernel.1 = (bf16[192,256]{1,0:T(8,128)(2,1)}, bf16[192,256]{1,0:T(8,128)(2,1)}, bf16[192,256]{1,0:T(8,128)(2,1)}, bf16[192,256]{1,0:T(8,128)(2,1)}) custom-call(s32[1,1,16]{2,1,0:T(1,128)} %ids.7, s32[1,1]{1,0:T(1,128)S(6)} %copy.13.counts, s32[1,256]{1,0:T(1,128)} %bitcast.9, bf16[1,1,16,256,256]{4,3,2,1,0:T(8,128)(2,1)} %tiles.5, ...), custom_call_target="tpu_custom_call" | custom-call | tf_op jit(solution)/shard_map/solve_kernel/pallas_call | solution.py:347
  63.0 1.3 %collective-permute-start.3 = (bf16[192,256]{1,0:T(8,128)(2,1)}, bf16[192,256]{1,0:T(8,128)(2,1)S(1)}, u32[]{:S(2)}, u32[]{:S(2)}) collective-permute-start(bf16[192,256]{1,0:T(8,128)(2,1)} %get-tuple-element.21.l1), channel_id=1, source_target_pairs={{0,8},{32,40},{64,72},{96,104},{128,136},{160,168},{192,200},{224,... | collective-permute-start | bytes 294920 | tf_op jit(solution)/shard_map/ppermute | solution.py:400
  64.3 0.7 collective-permute-start.2
  64.9 0.7 collective-permute-start.1
  65.6 4.4 %collective-permute-done.3 = bf16[192,256]{1,0:T(8,128)(2,1)S(1)} collective-permute-done((bf16[192,256]{1,0:T(8,128)(2,1)}, bf16[192,256]{1,0:T(8,128)(2,1)S(1)}, u32[]{:S(2)}, u32[]{:S(2)}) %collective-permute-start.3) | collective-permute-done | bytes 98336 | tf_op jit(solution)/shard_map/ppermute | solution.py:400
  70.0 0.0 collective-permute-done.2
  70.0 1.5 %collective-permute-start.4 = (bf16[192,256]{1,0:T(8,128)(2,1)S(1)}, bf16[192,256]{1,0:T(8,128)(2,1)S(1)}, u32[]{:S(2)}, u32[]{:S(2)}) collective-permute-start(bf16[192,256]{1,0:T(8,128)(2,1)S(1)} %select_select_fusion), channel_id=1, source_target_pairs={{0,4},{8,12},{16,20},{24,28},{32,36},{40,44},{48,52},{56,60},{64,6... | collective-permute-start | bytes 294920 | tf_op jit(solution)/shard_map/ppermute | solution.py:403
  71.5 1.9 %collective-permute-start.7 = (bf16[8,256]{1,0:T(8,128)(2,1)S(1)}, bf16[8,256]{1,0:T(8,128)(2,1)S(1)}, u32[]{:S(2)}, u32[]{:S(2)}) collective-permute-start(bf16[8,256]{1,0:T(8,128)(2,1)S(1)} %bitcast.4), channel_id=1, source_target_pairs={{0,4},{1,5},{2,6},{3,7},{4,0},{5,1},{6,2},{7,3},{8,12},{9,13},{10,... | collective-permute-start | bytes 12296 | tf_op jit(solution)/shard_map/ppermute | solution.py:405
  73.5 0.2 collective-permute-done.4
  73.7 4.3 %collective-permute-start.5 = (bf16[192,256]{1,0:T(8,128)(2,1)S(1)}, bf16[192,256]{1,0:T(8,128)(2,1)S(1)}, u32[]{:S(2)}, u32[]{:S(2)}) collective-permute-start(bf16[192,256]{1,0:T(8,128)(2,1)S(1)} %broadcast_select_fusion), channel_id=1, source_target_pairs={{0,2},{4,6},{8,10},{12,14},{16,18},{20,22},{24,26},{28,30},{32,34}... | collective-permute-start | bytes 294920 | tf_op jit(solution)/shard_map/ppermute | solution.py:403
  78.0 2.9 %collective-permute-done.7 = bf16[8,256]{1,0:T(8,128)(2,1)S(1)} collective-permute-done((bf16[8,256]{1,0:T(8,128)(2,1)S(1)}, bf16[8,256]{1,0:T(8,128)(2,1)S(1)}, u32[]{:S(2)}, u32[]{:S(2)}) %collective-permute-start.7) | collective-permute-done | bytes 4128 | tf_op jit(solution)/shard_map/ppermute | solution.py:405
  81.0 1.9 %collective-permute-start.8 = (bf16[16,256]{1,0:T(8,128)(2,1)S(1)}, bf16[16,256]{1,0:T(8,128)(2,1)S(1)}, u32[]{:S(2)}, u32[]{:S(2)}) collective-permute-start(bf16[16,256]{1,0:T(8,128)(2,1)S(1)} %pad_maximum_fusion.1), channel_id=1, source_target_pairs={{0,2},{1,3},{2,0},{3,1},{4,6},{5,7},{6,4},{7,5},{8,10},{9,11},{10,... | collective-permute-start | bytes 24584 | tf_op jit(solution)/shard_map/ppermute | solution.py:405
  82.9 0.0 collective-permute-done.5
  82.9 1.3 %collective-permute-start.6 = (bf16[192,256]{1,0:T(8,128)(2,1)S(1)}, bf16[192,256]{1,0:T(8,128)(2,1)S(1)}, u32[]{:S(2)}, u32[]{:S(2)}) collective-permute-start(bf16[192,256]{1,0:T(8,128)(2,1)S(1)} %broadcast_select_fusion.1), channel_id=1, source_target_pairs={{0,1},{2,3},{4,5},{6,7},{8,9},{10,11},{12,13},{14,15},{16,17},{18,... | collective-permute-start | bytes 294920 | tf_op jit(solution)/shard_map/ppermute | solution.py:403
  84.2 3.2 %collective-permute-done.8 = bf16[16,256]{1,0:T(8,128)(2,1)S(1)} collective-permute-done((bf16[16,256]{1,0:T(8,128)(2,1)S(1)}, bf16[16,256]{1,0:T(8,128)(2,1)S(1)}, u32[]{:S(2)}, u32[]{:S(2)}) %collective-permute-start.8) | collective-permute-done | bytes 8224 | tf_op jit(solution)/shard_map/ppermute | solution.py:405
  87.4 1.9 %collective-permute-start.9 = (bf16[32,256]{1,0:T(8,128)(2,1)S(1)}, bf16[32,256]{1,0:T(8,128)(2,1)S(1)}, u32[]{:S(2)}, u32[]{:S(2)}) collective-permute-start(bf16[32,256]{1,0:T(8,128)(2,1)S(1)} %pad_maximum_fusion), channel_id=1, source_target_pairs={{0,1},{1,0},{2,3},{3,2},{4,5},{5,4},{6,7},{7,6},{8,9},{9,8},{10,11... | collective-permute-start | bytes 49160 | tf_op jit(solution)/shard_map/ppermute | solution.py:405
  89.3 0.0 collective-permute-done.6
  89.4 3.6 %collective-permute-done.9 = bf16[32,256]{1,0:T(8,128)(2,1)S(1)} collective-permute-done((bf16[32,256]{1,0:T(8,128)(2,1)S(1)}, bf16[32,256]{1,0:T(8,128)(2,1)S(1)}, u32[]{:S(2)}, u32[]{:S(2)}) %collective-permute-start.9) | collective-permute-done | bytes 16416 | tf_op jit(solution)/shard_map/ppermute | solution.py:405
  93.0 0.8 broadcast_in_dim.14
  93.9 8.3 %all-to-all-start.2 = ((bf16[4,256,256]{2,1,0:T(8,128)(2,1)}), bf16[4,256,256]{2,1,0:T(8,128)(2,1)S(1)}, u32[]{:S(2)}, u32[]{:S(2)}) async-start(bf16[4,256,256]{2,1,0:T(8,128)(2,1)} %broadcast_in_dim.14), calls=%async_computation.2 | async-start | bytes 1048576 | tf_op jit(solution)/shard_map/all_to_all | solution.py:408
  102.1 5.3 %ready_kernel.1 = (bf16[16,256,256]{2,1,0:T(8,128)(2,1)}, bf16[4,256,256]{2,1,0:T(8,128)(2,1)}) custom-call(s32[1,1,16]{2,1,0:T(1,128)} %ids.7, s32[1,1]{1,0:T(1,128)S(6)} %copy.13.counts, s32[1,256]{1,0:T(1,128)} %bitcast.10, bf16[1,1,16,256,256]{4,3,2,1,0:T(8,128)(2,1)} %tiles.5, bf16[8,128,256]{2,1,0:T(8,128)(2,1)} %give_kernel.1.gave, ...), custom_call_target="tpu_custom_call" | custom-call | tf_op jit(solution)/shard_map/ready_kernel/pallas_call | solution.py:347
  107.5 1.3 %all-to-all-done.2.panel = bf16[4,256,256]{2,1,0:T(8,128)(2,1)S(1)} async-done(((bf16[4,256,256]{2,1,0:T(8,128)(2,1)}), bf16[4,256,256]{2,1,0:T(8,128)(2,1)S(1)}, u32[]{:S(2)}, u32[]{:S(2)}) %all-to-all-start.2) | async-done | bytes 524320 | tf_op jit(solution)/shard_map/all_to_all | solution.py:408
  108.8 0.8 copy-done
  109.6 3.6 %trail_kernel.1 = bf16[1,1,16,256,256]{4,3,2,1,0:T(8,128)(2,1)} custom-call(s32[1,1,16]{2,1,0:T(1,128)} %ids.7, s32[1,1]{1,0:T(1,128)S(6)} %copy.13.counts, bf16[1,1,16,256,256]{4,3,2,1,0:T(8,128)(2,1)} %bitcast.3, bf16[4,256,256]{2,1,0:T(8,128)(2,1)} %get-tuple-element.25.new, bf16[4,256,256]{2,1,0:T(8,128)(2,1)} %copy-done), custom_call_target="tpu_custom_call", output_to_operand_aliasing={{}: (2, {})} | custom-call | tf_op jit(solution)/shard_map/trail_kernel/pallas_call | solution.py:347
  (15 shorter events, 0.1 us)
Async XLA Ops:
  21.1 20.6 %collective-permute-start = (bf16[144,256]{1,0:T(8,128)(2,1)}, bf16[144,256]{1,0:T(8,128)(2,1)S(1)}, u32[]{:S(2)}, u32[]{:S(2)}) collective-permute-start(bf16[144,256]{1,0:T(8,128)(2,1)} %cross_kernel.1), channel_id=1, source_target_pairs={{0,64},{64,0},{1,65},{65,1},{2,66},{66,2},{3,67},{67,3},{4,68},{68... | collective-permute-start | bytes 221192 | tf_op jit(solution)/shard_map/ppermute | solution.py:378
  41.7 0.6 copy-start.1
  44.8 26.7 %copy-start.2 = (bf16[256,8]{0,1:T(8,128)(2,1)S(1)}, bf16[256,8]{0,1:T(8,128)(2,1)}, u32[]{:S(2)}) copy-start(bf16[256,8]{0,1:T(8,128)(2,1)} %param.10) | copy-start | bytes 12292
  63.0 7.0 %collective-permute-start.3 = (bf16[192,256]{1,0:T(8,128)(2,1)}, bf16[192,256]{1,0:T(8,128)(2,1)S(1)}, u32[]{:S(2)}, u32[]{:S(2)}) collective-permute-start(bf16[192,256]{1,0:T(8,128)(2,1)} %get-tuple-element.21.l1), channel_id=1, source_target_pairs={{0,8},{32,40},{64,72},{96,104},{128,136},{160,168},{192,200},{224,... | collective-permute-start | bytes 294920 | tf_op jit(solution)/shard_map/ppermute | solution.py:400
  64.3 5.7 %collective-permute-start.2 = (bf16[192,256]{1,0:T(8,128)(2,1)}, bf16[192,256]{1,0:T(8,128)(2,1)S(1)}, u32[]{:S(2)}, u32[]{:S(2)}) collective-permute-start(bf16[192,256]{1,0:T(8,128)(2,1)} %get-tuple-element.22.l2), channel_id=1, source_target_pairs={{0,16},{32,48},{64,80},{96,112},{128,144},{160,176},{192,208},{224... | collective-permute-start | bytes 294920 | tf_op jit(solution)/shard_map/ppermute | solution.py:400
  64.9 5.1 %collective-permute-start.1 = (bf16[192,256]{1,0:T(8,128)(2,1)}, bf16[192,256]{1,0:T(8,128)(2,1)S(1)}, u32[]{:S(2)}, u32[]{:S(2)}) collective-permute-start(bf16[192,256]{1,0:T(8,128)(2,1)} %get-tuple-element.23.l3), channel_id=1, source_target_pairs={{0,24},{32,56},{64,88},{96,120},{128,152},{160,184},{192,216},{224... | collective-permute-start | bytes 294920 | tf_op jit(solution)/shard_map/ppermute | solution.py:400
  70.0 3.7 %collective-permute-start.4 = (bf16[192,256]{1,0:T(8,128)(2,1)S(1)}, bf16[192,256]{1,0:T(8,128)(2,1)S(1)}, u32[]{:S(2)}, u32[]{:S(2)}) collective-permute-start(bf16[192,256]{1,0:T(8,128)(2,1)S(1)} %select_select_fusion), channel_id=1, source_target_pairs={{0,4},{8,12},{16,20},{24,28},{32,36},{40,44},{48,52},{56,60},{64,6... | collective-permute-start | bytes 294920 | tf_op jit(solution)/shard_map/ppermute | solution.py:403
  71.5 9.4 %collective-permute-start.7 = (bf16[8,256]{1,0:T(8,128)(2,1)S(1)}, bf16[8,256]{1,0:T(8,128)(2,1)S(1)}, u32[]{:S(2)}, u32[]{:S(2)}) collective-permute-start(bf16[8,256]{1,0:T(8,128)(2,1)S(1)} %bitcast.4), channel_id=1, source_target_pairs={{0,4},{1,5},{2,6},{3,7},{4,0},{5,1},{6,2},{7,3},{8,12},{9,13},{10,... | collective-permute-start | bytes 12296 | tf_op jit(solution)/shard_map/ppermute | solution.py:405
  73.7 9.2 %collective-permute-start.5 = (bf16[192,256]{1,0:T(8,128)(2,1)S(1)}, bf16[192,256]{1,0:T(8,128)(2,1)S(1)}, u32[]{:S(2)}, u32[]{:S(2)}) collective-permute-start(bf16[192,256]{1,0:T(8,128)(2,1)S(1)} %broadcast_select_fusion), channel_id=1, source_target_pairs={{0,2},{4,6},{8,10},{12,14},{16,18},{20,22},{24,26},{28,30},{32,34}... | collective-permute-start | bytes 294920 | tf_op jit(solution)/shard_map/ppermute | solution.py:403
  81.0 6.4 %collective-permute-start.8 = (bf16[16,256]{1,0:T(8,128)(2,1)S(1)}, bf16[16,256]{1,0:T(8,128)(2,1)S(1)}, u32[]{:S(2)}, u32[]{:S(2)}) collective-permute-start(bf16[16,256]{1,0:T(8,128)(2,1)S(1)} %pad_maximum_fusion.1), channel_id=1, source_target_pairs={{0,2},{1,3},{2,0},{3,1},{4,6},{5,7},{6,4},{7,5},{8,10},{9,11},{10,... | collective-permute-start | bytes 24584 | tf_op jit(solution)/shard_map/ppermute | solution.py:405
  82.9 6.4 %collective-permute-start.6 = (bf16[192,256]{1,0:T(8,128)(2,1)S(1)}, bf16[192,256]{1,0:T(8,128)(2,1)S(1)}, u32[]{:S(2)}, u32[]{:S(2)}) collective-permute-start(bf16[192,256]{1,0:T(8,128)(2,1)S(1)} %broadcast_select_fusion.1), channel_id=1, source_target_pairs={{0,1},{2,3},{4,5},{6,7},{8,9},{10,11},{12,13},{14,15},{16,17},{18,... | collective-permute-start | bytes 294920 | tf_op jit(solution)/shard_map/ppermute | solution.py:403
  87.4 5.6 %collective-permute-start.9 = (bf16[32,256]{1,0:T(8,128)(2,1)S(1)}, bf16[32,256]{1,0:T(8,128)(2,1)S(1)}, u32[]{:S(2)}, u32[]{:S(2)}) collective-permute-start(bf16[32,256]{1,0:T(8,128)(2,1)S(1)} %pad_maximum_fusion), channel_id=1, source_target_pairs={{0,1},{1,0},{2,3},{3,2},{4,5},{5,4},{6,7},{7,6},{8,9},{9,8},{10,11... | collective-permute-start | bytes 49160 | tf_op jit(solution)/shard_map/ppermute | solution.py:405
  93.9 14.9 %all-to-all-start.2 = ((bf16[4,256,256]{2,1,0:T(8,128)(2,1)}), bf16[4,256,256]{2,1,0:T(8,128)(2,1)S(1)}, u32[]{:S(2)}, u32[]{:S(2)}) async-start(bf16[4,256,256]{2,1,0:T(8,128)(2,1)} %broadcast_in_dim.14), calls=%async_computation.2 | async-start | bytes 1048576 | tf_op jit(solution)/shard_map/all_to_all | solution.py:408
  108.8 0.8 copy-start
where the time goes:
time: 114 us; the launch traced here: 113 us
  starting transfers between devices  39.4 us (35%)
  blocking collectives  30.9 us (27%)
  waiting for transfers between devices  20.5 us (18%)
  Pallas kernels  19 us (17%)
  local copies, waits for them, and re-layouts  2.28 us (2%)
    pallas_call x6, Pallas kernels, call(): pl.pallas_call(kernel, out_shape=shapes if several else shapes[0], in_spe...  19 us
    all_to_all x1, blocking collectives, body(): have = lax.all_to_all(relayed, plane, 0, 0, tiled=True)  16.1 us
    ppermute x1, starting transfers between devices, body(): theirs = lax.ppermute(crossing, 'zh', [(0, 1), (1, 0)])  15.7 us
    all_to_all x1, blocking collectives, body(): got = lax.all_to_all(gave, plane, 0, 0, tiled=True)  14.8 us
    ppermute x3, waiting for transfers between devices, body(): more = lax.ppermute(pieces, 'zl', [(a, a ^ step) for a in range(N_Z)])  9.75 us
    all_to_all x1, starting transfers between devices, body(): lax.all_to_all(jnp.broadcast_to(block[None], (N_X, SIDE, SIDE)), 'x', 0,...  8.28 us
    ppermute x3, starting transfers between devices, body(): lax.ppermute(part, 'zl', [(a, a + step) for a in range(0, N_Z, 2 * step)])  7.06 us
    ppermute x3, starting transfers between devices, body(): more = lax.ppermute(pieces, 'zl', [(a, a ^ step) for a in range(N_Z)])  5.74 us
  transfers between devices with their start and end apart: 11, of which 7 were waited for; matrix products, arithmetic and copies ran while one was open for 0% of the time, Pallas kernels for 5%

commit v1 on v0

--- a/solution.py
+++ b/solution.py
@@ -90,7 +90,7 @@
         @pl.when(wanted)
         def _():
             here[i, k] = 1
-            pltpu.make_async_copy(tiles.at[0, 0, s], held.at[k, i], sems.at[s]).start()
+            pltpu.make_async_copy(tiles.at[0, 0, s], held.at[k, i], sems.at[k, i]).start()
 
     for i in range(LOWER + 1):
         for k in range(LISTED):
@@ -106,14 +106,13 @@
     picks.append(hot(jnp.where(leaves, sub, piv - SIDE * p) == lane))
     pick = jnp.concatenate(picks, axis=1)
 
-    for s in range(SLOTS):
-        wanted, i, k = place(s)
-
-        @pl.when(wanted)
-        def _():
-            pltpu.make_async_copy(tiles.at[0, 0, s], held.at[k, i], sems.at[s]).wait()
-
     for k in range(LISTED):
+        for i in range(LOWER + 1):
+
+            @pl.when(here[i, k] == 1)
+            def _():
+                pltpu.make_async_copy(tiles.at[0, 0, 0], held.at[k, i], sems.at[k, i]).wait()
+
         rows = times(pick, held[k].reshape((LOWER + 1) * SIDE, SIDE)).astype(BF)
         out[:, k * CHUNK : (k + 1) * CHUNK] = rows.reshape(N_PLANE, CHUNK, SIDE)
 
@@ -136,24 +135,32 @@
     out[GIVEN:] = upper[...]
 
 
-def relay_kernel(pivots, got, theirs, upper, out):
-    zh = lax.axis_index("zh")
+def wide(v):
+    return jnp.broadcast_to(v[None], (N_PLANE, CHUNK, SIDE)).reshape(SIDE, SIDE)
+
+
+def relay_plan(pivots):
     near, place = chunk_owner(pivots)
-
-    def wide(v):
-        v = jnp.where(v, 1, 0) if v.dtype == jnp.bool_ else v
-        return jnp.broadcast_to(v[None], (N_PLANE, CHUNK, SIDE)).reshape(SIDE, SIDE)
-
-    near, place = wide(near) == 1, wide(place)
+    near, place = wide(jnp.where(near, 1, 0)) == 1, wide(place)
+    mine = iota(0) // CHUNK == place
+    far = jnp.logical_not(near) | (mine & (lax.axis_index("zh") == 1))
+    return far, jnp.where(mine, 0, place)
+
+
+def near_kernel(pivots, got, out):
+    far, source = relay_plan(pivots)
     to, frm = iota(0), iota(1)
-    mine = to // CHUNK == place
-    far = jnp.logical_not(near) | (mine & (zh == 1))
-    source = jnp.where(mine, 0, place)
     pick = hot((to % CHUNK == frm % CHUNK) & (frm // CHUNK == source) & jnp.logical_not(far))
     for k in range(LISTED):
-        other = theirs[k * CHUNK : (k + 1) * CHUNK].astype(F32)
-        other = jnp.broadcast_to(other[None], (N_PLANE, CHUNK, SIDE)).reshape(SIDE, SIDE)
-        rows = jnp.where(far, other, times(pick, block_rows(got, k))).astype(BF)
+        out[k] = times(pick, block_rows(got, k)).astype(BF)
+
+
+def relay_kernel(pivots, near, theirs, upper, out):
+    zh = lax.axis_index("zh")
+    far, _ = relay_plan(pivots)
+    for k in range(LISTED):
+        other = wide(theirs[k * CHUNK : (k + 1) * CHUNK].astype(F32))
+        rows = jnp.where(far, other, near[k].astype(F32)).astype(BF)
         out[:, k * CHUNK : (k + 1) * CHUNK] = rows.reshape(N_PLANE, CHUNK, SIDE)
     ours, others = upper[...].astype(F32), theirs[GIVEN:].astype(F32)
     for h in range(2):
@@ -163,68 +170,87 @@
         )
 
 
-def swap_in(pivots, old, tile, first):
+def swap_plan(pivots, first):
     match = pivots - first == iota(0)
-    moved = jnp.max(jnp.where(match, 1.0, 0.0), axis=1, keepdims=True) > 0.0
-    return jnp.where(moved, times(hot(match), old), tile.astype(F32)).astype(BF)
+    return hot(match), jnp.max(jnp.where(match, 1.0, 0.0), axis=1, keepdims=True) > 0.0
+
+
+def swap_in(plan, old, tile):
+    return jnp.where(plan[1], times(plan[0], old), tile.astype(F32)).astype(BF)
 
 
 def solve_kernel(ids, counts, pivots, tiles, got, *rest):
-    outs, (inverse, old, held, here, sems) = rest[:N_X], rest[N_X:]
+    outs, (inverse, old, held, swapped, here, sems, olds, inverses) = rest[:N_X], rest[N_X:]
     p, q = row_of(), col_of()
 
     @pl.when(q == 0)
     def _():
+        copies = []
+        for j in range(N_PLANE):
+            rows = pl.ds(j * CHUNK, CHUNK)
+            copies.append(
+                pltpu.make_async_copy(got.at[j, pl.ds(UPPER * CHUNK, CHUNK)], old.at[rows], olds.at[j])
+            )
+        for j in range(N_ROW):
+            y, h, c = j // 4, j // 2 % 2, j % 2
+            rows = pl.ds(GIVEN + h * PIECE, PIECE)
+            copies.append(
+                pltpu.make_async_copy(
+                    got.at[2 * y + c, rows], inverse.at[pl.ds(j * PIECE, PIECE)], inverses.at[j]
+                )
+            )
         for i in range(LOWER + 1):
             here[i] = 0
-
-        def place(s):
+        for s in range(SLOTS):
             row, col, live = slot_of(ids, counts, s)
             top = (row == 0) & (p == 0)
             i = jnp.where(top, LOWER, ROWS - 1 - row)
-            return live & (col == 0) & (top | (row >= ROWS - LOWER)), i
-
-        for s in range(SLOTS):
-            wanted, i = place(s)
-
-            @pl.when(wanted)
+
+            @pl.when(live & (col == 0) & (top | (row >= ROWS - LOWER)))
             def _():
                 here[i] = 1
-                pltpu.make_async_copy(tiles.at[0, 0, s], held.at[i], sems.at[s]).start()
-
-        for y in range(N_Y):
-            for h in range(2):
-                for c in range(2):
-                    r = (4 * y + 2 * h + c) * PIECE
-                    a = GIVEN + h * PIECE
-                    inverse[r : r + PIECE] = got[2 * y + c, a : a + PIECE]
+                pltpu.make_async_copy(tiles.at[0, 0, s], held.at[i], sems.at[i]).start()
+
+        for copy in copies:
+            copy.start()
         piv = jnp.broadcast_to(pivots[...], (SIDE, SIDE))
-        old[...] = block_rows(got, UPPER)
-
-        for s in range(SLOTS):
-            wanted, i = place(s)
-
-            @pl.when(wanted)
-            def _():
-                pltpu.make_async_copy(tiles.at[0, 0, s], held.at[i], sems.at[s]).wait()
+        plans = [swap_plan(piv, SIDE * (p + N_ROW * (ROWS - 1 - i))) for i in range(LOWER)]
+        for copy in copies[:N_PLANE]:
+            copy.wait()
 
         @pl.when(here[LOWER] == 1)
         def _():
+            pltpu.make_async_copy(tiles.at[0, 0, 0], held.at[LOWER], sems.at[LOWER]).wait()
             old[...] = held[LOWER]
 
         for i in range(LOWER):
 
             @pl.when(here[i] == 1)
             def _():
-                swapped = swap_in(piv, old[...], held[i], SIDE * (p + N_ROW * (ROWS - 1 - i)))
-                solved = times(swapped, inverse[...]).astype(BF)
-                for c in range(N_X):
-                    outs[c][i * PART : (i + 1) * PART] = solved[c * PART : (c + 1) * PART]
+                pltpu.make_async_copy(tiles.at[0, 0, 0], held.at[i], sems.at[i]).wait()
 
             @pl.when(here[i] == 0)
             def _():
-                for c in range(N_X):
-                    outs[c][i * PART : (i + 1) * PART] = jnp.zeros((PART, SIDE), BF)
+                held[i] = jnp.zeros((SIDE, SIDE), BF)
+
+        for i in range(LOWER):
+            swapped[i * SIDE : (i + 1) * SIDE] = swap_in(plans[i], old[...], held[i])
+        for copy in copies[N_PLANE:]:
+            copy.wait()
+        solved = times(swapped[...], inverse[...]).astype(BF)
+        for i in range(LOWER):
+            for c in range(N_X):
+                a = i * SIDE + c * PART
+                outs[c][i * PART : (i + 1) * PART] = solved[a : a + PART]
+
+
+def fan_kernel(part, pieces, sent, out):
+    odd = lax.axis_index("zl") % 2 == 1
+    rows = jnp.where(odd, sent[:PANEL].astype(F32), part[...].astype(F32)).astype(BF)
+    for c in range(N_X):
+        out[c, :PANEL] = rows
+        out[c, PANEL : PANEL + PART // 2] = pieces[...]
+        out[c, PANEL + PART // 2 :] = sent[PANEL:]
 
 
 def ready_kernel(ids, counts, pivots, tiles, gave, got, l0, l1, l2, l3, out, new, old):
@@ -271,7 +297,7 @@
 
         @pl.when(is_swap)
         def _():
-            out[s] = swap_in(piv, old[k], tiles[0, 0, s], SIDE * (p + N_ROW * row))
+            out[s] = swap_in(swap_plan(piv, SIDE * (p + N_ROW * row)), old[k], tiles[0, 0, s])
 
         @pl.when(is_kept)
         def _():
@@ -341,13 +367,17 @@
             pltpu.make_async_copy(held.at[s], out.at[0, 0, s], back.at[s]).wait()
 
 
-def call(kernel, specs, ins, shapes, scratch=(), out_space=VMEM, aliases=None):
-    shapes = [jax.ShapeDtypeStruct(o, BF) for o in shapes]
+def call(kernel, specs, ins, shapes, scratch=(), out_space=VMEM, aliases=None, kept=True):
+    shapes = [pltpu.VMEM(o, BF) if kept else jax.ShapeDtypeStruct(o, BF) for o in shapes]
     several = len(shapes) > 1
+    ins = [
+        pltpu.with_memory_space_constraint(a, pltpu.VMEM) if c == "v" else a
+        for c, a in zip(specs, ins, strict=True)
+    ]
     return pl.pallas_call(
         kernel,
         out_shape=shapes if several else shapes[0],
-        in_specs=[{"s": SMEM, "v": VMEM, "a": ANY}[c] for c in specs],
+        in_specs=[{"s": SMEM, "v": VMEM, "w": VMEM, "a": ANY}[c] for c in specs],
         out_specs=[out_space] * len(shapes) if several else out_space,
         scratch_shapes=list(scratch),
         input_output_aliases=aliases or {},
@@ -364,61 +394,68 @@
 
     gave = call(
         give_kernel,
-        "ssva",
+        "sswa",
         [tile_ids, counts, lanes, tiles],
         [(N_PLANE, GIVEN, SIDE)],
         [
             pltpu.VMEM((LISTED, LOWER + 1, SIDE, SIDE), BF),
             pltpu.SMEM((LOWER + 1, LISTED), jnp.int32),
-            pltpu.SemaphoreType.DMA((SLOTS,)),
+            pltpu.SemaphoreType.DMA((LISTED, LOWER + 1)),
         ],
     )
     got = lax.all_to_all(gave, plane, 0, 0, tiled=True)
-    crossing = call(cross_kernel, "svv", [pivots, got, u_inverse], [(GIVEN + PIECE, SIDE)])
+    crossing = call(cross_kernel, "svw", [pivots, got, u_inverse], [(GIVEN + PIECE, SIDE)])
     theirs = lax.ppermute(crossing, "zh", [(0, 1), (1, 0)])
+    near = call(near_kernel, "sv", [pivots, got], [(LISTED, SIDE, SIDE)])
     relayed = call(
-        relay_kernel, "svvv", [pivots, got, theirs, u_inverse], [(N_PLANE, SENT, SIDE)]
+        relay_kernel, "svvw", [pivots, near, theirs, u_inverse], [(N_PLANE, SENT, SIDE)]
     )
     have = lax.all_to_all(relayed, plane, 0, 0, tiled=True)
+    have, pieces = lax.optimization_barrier((have, l_inverse.T))
 
     parts = call(
         solve_kernel,
-        "ssvav",
+        "sswaa",
         [tile_ids, counts, lanes, tiles, have],
         [(PANEL, SIDE)] * N_X,
         [
             pltpu.VMEM(tile, BF),
             pltpu.VMEM(tile, BF),
             pltpu.VMEM((LOWER + 1, SIDE, SIDE), BF),
+            pltpu.VMEM((LOWER * SIDE, SIDE), BF),
             pltpu.SMEM((LOWER + 1,), jnp.int32),
-            pltpu.SemaphoreType.DMA((SLOTS,)),
+            pltpu.SemaphoreType.DMA((LOWER + 1,)),
+            pltpu.SemaphoreType.DMA((N_PLANE,)),
+            pltpu.SemaphoreType.DMA((N_ROW,)),
         ],
     )
-    *parts, pieces = lax.optimization_barrier((*parts, l_inverse.T))
     part = parts[0]
     for c in range(1, N_X):
         sent = lax.ppermute(parts[c], PCOL, [(0, c * N_Z)])
         part = jnp.where(x == c, sent, part)
-    for step in (4, 2, 1):
-        sent = lax.ppermute(part, "zl", [(a, a + step) for a in range(0, N_Z, 2 * step)])
-        part = jnp.where(z % (2 * step) == step, sent, part)
+    first = part
+    for step in (4, 2):
         more = lax.ppermute(pieces, "zl", [(a, a ^ step) for a in range(N_Z)])
         pieces = jnp.concatenate([pieces, more], axis=0)
+    for to in (6, 4, 2):
+        sent = lax.ppermute(first, "zl", [(0, to)])
+        part = jnp.where(z == to, sent, part)
     block = jnp.concatenate([part, pieces], axis=0)
-    panel = lax.all_to_all(
-        jnp.broadcast_to(block[None], (N_X, SIDE, SIDE)), "x", 0, 0, tiled=True
-    )
+    sent = lax.ppermute(block, "zl", [(a, a ^ 1) for a in range(N_Z)])
+    fan = call(fan_kernel, "vvv", [part, pieces, sent], [(N_X, SIDE, SIDE)])
+    panel = lax.all_to_all(fan, "x", 0, 0, tiled=True)
 
     ready, new = call(
         ready_kernel,
-        "ssvvvvvvvv",
+        "sswwwwwwww",
         [tile_ids, counts, lanes, tiles, gave, have, *parts],
         [(SLOTS, SIDE, SIDE), (LISTED, SIDE, SIDE)],
         [pltpu.VMEM((LISTED, SIDE, SIDE), BF)],
+        kept=False,
     )
     return call(
         trail_kernel,
-        "ssavv",
+        "ssawv",
         [tile_ids, counts, ready[None, None], new, panel],
         [(1, 1, SLOTS, SIDE, SIDE)],
         [
@@ -430,6 +467,7 @@
         ],
         out_space=ANY,
         aliases={2: 0},
+        kept=False,
     )
 
 

time: 114 us -> 105 us (0.921)
  the two profiles are of different devices: /device:TPU:2 before, /device:TPU:8 now
where the time goes in v1:
time: 105 us; the launch traced here: 106 us
  starting transfers between devices  37.4 us (36%)
  blocking collectives  32.1 us (31%)
  Pallas kernels  22.4 us (21%)
  waiting for transfers between devices  12.6 us (12%)
    pallas_call x8, Pallas kernels, call(): pl.pallas_call(kernel, out_shape=shapes if several else shapes[0], in_spe...  22.4 us
    all_to_all x1, blocking collectives, body(): got = lax.all_to_all(gave, plane, 0, 0, tiled=True)  17.2 us
    all_to_all x1, blocking collectives, body(): have = lax.all_to_all(relayed, plane, 0, 0, tiled=True)  14.9 us
    ppermute x1, starting transfers between devices, body(): theirs = lax.ppermute(crossing, 'zh', [(0, 1), (1, 0)])  12.2 us
    ppermute x3, starting transfers between devices, body(): sent = lax.ppermute(first, 'zl', [(0, to)])  9.59 us
    ppermute x3, starting transfers between devices, body(): sent = lax.ppermute(parts[c], PCOL, [(0, c * N_Z)])  6.47 us
    ppermute x1, waiting for transfers between devices, body(): sent = lax.ppermute(block, 'zl', [(a, a ^ 1) for a in range(N_Z)])  4.75 us
    ppermute x2, waiting for transfers between devices, body(): more = lax.ppermute(pieces, 'zl', [(a, a ^ step) for a in range(N_Z)])  4.02 us
  transfers between devices with their start and end apart: 11, of which 6 were waited for; matrix products, arithmetic and copies ran while one was open for 0% of the time, Pallas kernels for 7%

profile of v1, /device:TPU:8, one launch (start us, length us, event | category | flops | bytes accessed | tf_op | source)
XLA Modules:
  0.0 105.5 jit_solution(18205200952270460532)
XLA Ops:
  0.7 3.8 %give_kernel.1.gave = bf16[8,128,256]{2,1,0:T(8,128)(2,1)S(1)} custom-call(s32[1,1,16]{2,1,0:T(1,128)} %ids.7, s32[1,1]{1,0:T(1,128)S(6)} %copy.9.counts, s32[1,256]{1,0:T(1,128)} %bitcast.8, bf16[1,1,16,256,256]{4,3,2,1,0:T(8,128)(2,1)} %tiles.5), custom_call_target="tpu_custom_call" | custom-call | tf_op jit(solution)/shard_map/give_kernel/pallas_call | solution.py:377
  4.5 17.2 %all_to_all.15.got = bf16[8,128,256]{2,1,0:T(8,128)(2,1)S(1)} all-to-all(bf16[8,128,256]{2,1,0:T(8,128)(2,1)S(1)} %give_kernel.1.gave), channel_id=1, replica_groups=mesh['y'=4,'zh'=2,'core'=2,'x'=4,'zl'=8] {'y','core'}, dimensions={0} | all-to-all | bytes 1048576 | tf_op jit(solution)/shard_map/all_to_all | solution.py:406
  21.7 1.1 %cross_kernel.1 = bf16[144,256]{1,0:T(8,128)(2,1)S(1)} custom-call(s32[256]{0:T(256)} %pivots.5, bf16[8,128,256]{2,1,0:T(8,128)(2,1)S(1)} %all_to_all.15.got, bf16[16,256]{1,0:T(8,128)(2,1)} %upper.3), custom_call_target="tpu_custom_call" | custom-call | tf_op jit(solution)/shard_map/cross_kernel/pallas_call | solution.py:377
  22.8 12.2 %collective-permute-start = (bf16[144,256]{1,0:T(8,128)(2,1)S(1)}, bf16[144,256]{1,0:T(8,128)(2,1)S(1)}, u32[]{:S(2)}, u32[]{:S(2)}) collective-permute-start(bf16[144,256]{1,0:T(8,128)(2,1)S(1)} %cross_kernel.1), channel_id=1, source_target_pairs={{0,64},{64,0},{1,65},{65,1},{2,66},{66,2},{3,67},{67,3},{4,68},{68... | collective-permute-start | bytes 221192 | tf_op jit(solution)/shard_map/ppermute | solution.py:408
  35.0 1.2 %near_kernel.1.near = bf16[4,256,256]{2,1,0:T(8,128)(2,1)S(1)} custom-call(s32[256]{0:T(256)} %pivots.5, bf16[8,128,256]{2,1,0:T(8,128)(2,1)S(1)} %all_to_all.15.got), custom_call_target="tpu_custom_call" | custom-call | tf_op jit(solution)/shard_map/near_kernel/pallas_call | solution.py:377
  36.2 1.7 %collective-permute-done.theirs = bf16[144,256]{1,0:T(8,128)(2,1)S(1)} collective-permute-done((bf16[144,256]{1,0:T(8,128)(2,1)S(1)}, bf16[144,256]{1,0:T(8,128)(2,1)S(1)}, u32[]{:S(2)}, u32[]{:S(2)}) %collective-permute-start) | collective-permute-done | bytes 73760 | tf_op jit(solution)/shard_map/ppermute | solution.py:408
  37.9 1.0 relay_kernel.1
  38.9 0.0 copy-start.5
  39.0 14.9 %all_to_all.16.got = bf16[8,160,256]{2,1,0:T(8,128)(2,1)} all-to-all(bf16[8,160,256]{2,1,0:T(8,128)(2,1)S(1)} %relay_kernel.1), channel_id=1, replica_groups=mesh['y'=4,'zh'=2,'core'=2,'x'=4,'zl'=8] {'y','core'}, dimensions={0} | all-to-all | bytes 1310720 | tf_op jit(solution)/shard_map/all_to_all | solution.py:413
  53.8 3.0 %solve_kernel.1 = (bf16[192,256]{1,0:T(8,128)(2,1)S(1)}, bf16[192,256]{1,0:T(8,128)(2,1)S(1)}, bf16[192,256]{1,0:T(8,128)(2,1)S(1)}, bf16[192,256]{1,0:T(8,128)(2,1)S(1)}) custom-call(s32[1,1,16]{2,1,0:T(1,128)} %ids.7, s32[1,1]{1,0:T(1,128)S(6)} %copy.9.counts, s32[1,256]{1,0:T(1,128)} %bitcast.9, bf16[1,1,16,256,256]{4,3,2,1,0:T(8,128)(2,1)} %tiles.5, ...), custom_call_target="tpu_custom_call" | custom-call | tf_op jit(solution)/shard_map/solve_kernel/pallas_call | solution.py:377
  56.9 3.1 %collective-permute-start.3 = (bf16[192,256]{1,0:T(8,128)(2,1)S(1)}, bf16[192,256]{1,0:T(8,128)(2,1)S(1)}, u32[]{:S(2)}, u32[]{:S(2)}) collective-permute-start(bf16[192,256]{1,0:T(8,128)(2,1)S(1)} %get-tuple-element.15.l1), channel_id=1, source_target_pairs={{0,8},{32,40},{64,72},{96,104},{128,136},{160,168},{192,200},{224,... | collective-permute-start | bytes 294920 | tf_op jit(solution)/shard_map/ppermute | solution.py:434
  59.9 2.1 %collective-permute-start.2 = (bf16[192,256]{1,0:T(8,128)(2,1)S(1)}, bf16[192,256]{1,0:T(8,128)(2,1)S(1)}, u32[]{:S(2)}, u32[]{:S(2)}) collective-permute-start(bf16[192,256]{1,0:T(8,128)(2,1)S(1)} %get-tuple-element.16.l2), channel_id=1, source_target_pairs={{0,16},{32,48},{64,80},{96,112},{128,144},{160,176},{192,208},{224... | collective-permute-start | bytes 294920 | tf_op jit(solution)/shard_map/ppermute | solution.py:434
  62.0 1.3 %collective-permute-start.1 = (bf16[192,256]{1,0:T(8,128)(2,1)S(1)}, bf16[192,256]{1,0:T(8,128)(2,1)S(1)}, u32[]{:S(2)}, u32[]{:S(2)}) collective-permute-start(bf16[192,256]{1,0:T(8,128)(2,1)S(1)} %get-tuple-element.17.l3), channel_id=1, source_target_pairs={{0,24},{32,56},{64,88},{96,120},{128,152},{160,184},{192,216},{224... | collective-permute-start | bytes 294920 | tf_op jit(solution)/shard_map/ppermute | solution.py:434
  63.4 1.9 %collective-permute-start.7 = (bf16[8,256]{1,0:T(8,128)(2,1)S(1)}, bf16[8,256]{1,0:T(8,128)(2,1)S(1)}, u32[]{:S(2)}, u32[]{:S(2)}) collective-permute-start(bf16[8,256]{1,0:T(8,128)(2,1)S(1)} %bitcast.4), channel_id=1, source_target_pairs={{0,4},{1,5},{2,6},{3,7},{4,0},{5,1},{6,2},{7,3},{8,12},{9,13},{10,... | collective-permute-start | bytes 12296 | tf_op jit(solution)/shard_map/ppermute | solution.py:438
  65.3 0.0 collective-permute-done.3
  65.3 0.0 collective-permute-done.2
  65.3 0.2 collective-permute-done.1
  65.6 4.4 %collective-permute-start.6 = (bf16[192,256]{1,0:T(8,128)(2,1)S(1)}, bf16[192,256]{1,0:T(8,128)(2,1)S(1)}, u32[]{:S(2)}, u32[]{:S(2)}) collective-permute-start(bf16[192,256]{1,0:T(8,128)(2,1)S(1)} %select_select_fusion.1), channel_id=1, source_target_pairs={{0,6},{8,14},{16,22},{24,30},{32,38},{40,46},{48,54},{56,62},{64,7... | collective-permute-start | bytes 294920 | tf_op jit(solution)/shard_map/ppermute | solution.py:441
  70.0 3.9 %collective-permute-start.5 = (bf16[192,256]{1,0:T(8,128)(2,1)S(1)}, bf16[192,256]{1,0:T(8,128)(2,1)S(1)}, u32[]{:S(2)}, u32[]{:S(2)}) collective-permute-start(bf16[192,256]{1,0:T(8,128)(2,1)S(1)} %select_select_fusion.1), channel_id=1, source_target_pairs={{0,4},{8,12},{16,20},{24,28},{32,36},{40,44},{48,52},{56,60},{64,6... | collective-permute-start | bytes 294920 | tf_op jit(solution)/shard_map/ppermute | solution.py:441
  73.9 1.3 %collective-permute-start.4 = (bf16[192,256]{1,0:T(8,128)(2,1)S(1)}, bf16[192,256]{1,0:T(8,128)(2,1)S(1)}, u32[]{:S(2)}, u32[]{:S(2)}) collective-permute-start(bf16[192,256]{1,0:T(8,128)(2,1)S(1)} %select_select_fusion.1), channel_id=1, source_target_pairs={{0,2},{8,10},{16,18},{24,26},{32,34},{40,42},{48,50},{56,58},{64,6... | collective-permute-start | bytes 294920 | tf_op jit(solution)/shard_map/ppermute | solution.py:441
  75.2 0.0 collective-permute-done.7
  75.2 1.9 %collective-permute-start.8 = (bf16[16,256]{1,0:T(8,128)(2,1)S(1)}, bf16[16,256]{1,0:T(8,128)(2,1)S(1)}, u32[]{:S(2)}, u32[]{:S(2)}) collective-permute-start(bf16[16,256]{1,0:T(8,128)(2,1)S(1)} %pad_maximum_fusion.2), channel_id=1, source_target_pairs={{0,2},{1,3},{2,0},{3,1},{4,6},{5,7},{6,4},{7,5},{8,10},{9,11},{10,... | collective-permute-start | bytes 24584 | tf_op jit(solution)/shard_map/ppermute | solution.py:438
  77.1 0.0 collective-permute-done.6
  77.1 0.5 collective-permute-done.4
  77.6 4.0 %collective-permute-done.8 = bf16[16,256]{1,0:T(8,128)(2,1)S(1)} collective-permute-done((bf16[16,256]{1,0:T(8,128)(2,1)S(1)}, bf16[16,256]{1,0:T(8,128)(2,1)S(1)}, u32[]{:S(2)}, u32[]{:S(2)}) %collective-permute-start.8) | collective-permute-done | bytes 8224 | tf_op jit(solution)/shard_map/ppermute | solution.py:438
  81.7 1.9 %collective-permute-start.9 = (bf16[224,256]{1,0:T(8,128)(2,1)S(1)}, bf16[224,256]{1,0:T(8,128)(2,1)S(1)}, u32[]{:S(2)}, u32[]{:S(2)}) collective-permute-start(bf16[224,256]{1,0:T(8,128)(2,1)S(1)} %pad_maximum_fusion), channel_id=1, source_target_pairs={{0,1},{1,0},{2,3},{3,2},{4,5},{5,4},{6,7},{7,6},{8,9},{9,8},{10,11... | collective-permute-start | bytes 344072 | tf_op jit(solution)/shard_map/ppermute | solution.py:444
  83.6 4.7 %collective-permute-done.9.sent = bf16[224,256]{1,0:T(8,128)(2,1)S(1)} collective-permute-done((bf16[224,256]{1,0:T(8,128)(2,1)S(1)}, bf16[224,256]{1,0:T(8,128)(2,1)S(1)}, u32[]{:S(2)}, u32[]{:S(2)}) %collective-permute-start.9) | collective-permute-done | bytes 114720 | tf_op jit(solution)/shard_map/ppermute | solution.py:444
  88.3 0.8 fan_kernel.1
  89.2 3.5 %all-to-all-start.2 = ((bf16[4,256,256]{2,1,0:T(8,128)(2,1)}), bf16[4,256,256]{2,1,0:T(8,128)(2,1)S(1)}, u32[]{:S(2)}, u32[]{:S(2)}) async-start(bf16[4,256,256]{2,1,0:T(8,128)(2,1)} %fan_kernel.1), calls=%async_computation.2 | async-start | bytes 1048576 | tf_op jit(solution)/shard_map/all_to_all | solution.py:446
  92.7 6.6 %ready_kernel.1 = (bf16[16,256,256]{2,1,0:T(8,128)(2,1)}, bf16[4,256,256]{2,1,0:T(8,128)(2,1)}) custom-call(s32[1,1,16]{2,1,0:T(1,128)} %ids.7, s32[1,1]{1,0:T(1,128)S(6)} %copy.9.counts, s32[1,256]{1,0:T(1,128)} %bitcast.10, bf16[1,1,16,256,256]{4,3,2,1,0:T(8,128)(2,1)} %tiles.5, bf16[8,128,256]{2,1,0:T(8,128)(2,1)} %copy-done, ...), custom_call_target="tpu_custom_call" | custom-call | tf_op jit(solution)/shard_map/ready_kernel/pallas_call | solution.py:377
  99.3 1.4 %all-to-all-done.2.panel = bf16[4,256,256]{2,1,0:T(8,128)(2,1)S(1)} async-done(((bf16[4,256,256]{2,1,0:T(8,128)(2,1)}), bf16[4,256,256]{2,1,0:T(8,128)(2,1)S(1)}, u32[]{:S(2)}, u32[]{:S(2)}) %all-to-all-start.2) | async-done | bytes 524320 | tf_op jit(solution)/shard_map/all_to_all | solution.py:446
  100.7 4.8 %trail_kernel.1 = bf16[1,1,16,256,256]{4,3,2,1,0:T(8,128)(2,1)} custom-call(s32[1,1,16]{2,1,0:T(1,128)} %ids.7, s32[1,1]{1,0:T(1,128)S(6)} %copy.9.counts, bf16[1,1,16,256,256]{4,3,2,1,0:T(8,128)(2,1)} %bitcast.3, bf16[4,256,256]{2,1,0:T(8,128)(2,1)} %get-tuple-element.19.new, ...), custom_call_target="tpu_custom_call", output_to_operand_aliasing={{}: (2, {})} | custom-call | tf_op jit(solution)/shard_map/trail_kernel/pallas_call | solution.py:377
  (17 shorter events, 0.1 us)
Async XLA Ops:
  4.4 49.4 %copy-start = (bf16[8,128,256]{2,1,0:T(8,128)(2,1)}, bf16[8,128,256]{2,1,0:T(8,128)(2,1)S(1)}, u32[]{:S(2)}) copy-start(bf16[8,128,256]{2,1,0:T(8,128)(2,1)S(1)} %give_kernel.1.gave) | copy-start | bytes 1572868
  22.8 15.1 %collective-permute-start = (bf16[144,256]{1,0:T(8,128)(2,1)S(1)}, bf16[144,256]{1,0:T(8,128)(2,1)S(1)}, u32[]{:S(2)}, u32[]{:S(2)}) collective-permute-start(bf16[144,256]{1,0:T(8,128)(2,1)S(1)} %cross_kernel.1), channel_id=1, source_target_pairs={{0,64},{64,0},{1,65},{65,1},{2,66},{66,2},{3,67},{67,3},{4,68},{68... | collective-permute-start | bytes 221192 | tf_op jit(solution)/shard_map/ppermute | solution.py:408
  38.9 24.4 %copy-start.5 = (bf16[256,8]{0,1:T(8,128)(2,1)S(1)}, bf16[256,8]{0,1:T(8,128)(2,1)}, u32[]{:S(2)}) copy-start(bf16[256,8]{0,1:T(8,128)(2,1)} %param.10) | copy-start | bytes 12292
  56.8 35.8 %copy-start.1 = (bf16[192,256]{1,0:T(8,128)(2,1)}, bf16[192,256]{1,0:T(8,128)(2,1)S(1)}, u32[]{:S(2)}) copy-start(bf16[192,256]{1,0:T(8,128)(2,1)S(1)} %get-tuple-element.14.l0) | copy-start | bytes 294916
  56.8 35.8 %copy-start.2 = (bf16[192,256]{1,0:T(8,128)(2,1)}, bf16[192,256]{1,0:T(8,128)(2,1)S(1)}, u32[]{:S(2)}) copy-start(bf16[192,256]{1,0:T(8,128)(2,1)S(1)} %get-tuple-element.15.l1) | copy-start | bytes 294916
  56.8 35.8 %copy-start.3 = (bf16[192,256]{1,0:T(8,128)(2,1)}, bf16[192,256]{1,0:T(8,128)(2,1)S(1)}, u32[]{:S(2)}) copy-start(bf16[192,256]{1,0:T(8,128)(2,1)S(1)} %get-tuple-element.16.l2) | copy-start | bytes 294916
  56.8 35.8 %copy-start.4 = (bf16[192,256]{1,0:T(8,128)(2,1)}, bf16[192,256]{1,0:T(8,128)(2,1)S(1)}, u32[]{:S(2)}) copy-start(bf16[192,256]{1,0:T(8,128)(2,1)S(1)} %get-tuple-element.17.l3) | copy-start | bytes 294916
  56.9 8.4 %collective-permute-start.3 = (bf16[192,256]{1,0:T(8,128)(2,1)S(1)}, bf16[192,256]{1,0:T(8,128)(2,1)S(1)}, u32[]{:S(2)}, u32[]{:S(2)}) collective-permute-start(bf16[192,256]{1,0:T(8,128)(2,1)S(1)} %get-tuple-element.15.l1), channel_id=1, source_target_pairs={{0,8},{32,40},{64,72},{96,104},{128,136},{160,168},{192,200},{224,... | collective-permute-start | bytes 294920 | tf_op jit(solution)/shard_map/ppermute | solution.py:434
  59.9 5.4 %collective-permute-start.2 = (bf16[192,256]{1,0:T(8,128)(2,1)S(1)}, bf16[192,256]{1,0:T(8,128)(2,1)S(1)}, u32[]{:S(2)}, u32[]{:S(2)}) collective-permute-start(bf16[192,256]{1,0:T(8,128)(2,1)S(1)} %get-tuple-element.16.l2), channel_id=1, source_target_pairs={{0,16},{32,48},{64,80},{96,112},{128,144},{160,176},{192,208},{224... | collective-permute-start | bytes 294920 | tf_op jit(solution)/shard_map/ppermute | solution.py:434
  62.0 3.5 %collective-permute-start.1 = (bf16[192,256]{1,0:T(8,128)(2,1)S(1)}, bf16[192,256]{1,0:T(8,128)(2,1)S(1)}, u32[]{:S(2)}, u32[]{:S(2)}) collective-permute-start(bf16[192,256]{1,0:T(8,128)(2,1)S(1)} %get-tuple-element.17.l3), channel_id=1, source_target_pairs={{0,24},{32,56},{64,88},{96,120},{128,152},{160,184},{192,216},{224... | collective-permute-start | bytes 294920 | tf_op jit(solution)/shard_map/ppermute | solution.py:434
  63.4 11.8 %collective-permute-start.7 = (bf16[8,256]{1,0:T(8,128)(2,1)S(1)}, bf16[8,256]{1,0:T(8,128)(2,1)S(1)}, u32[]{:S(2)}, u32[]{:S(2)}) collective-permute-start(bf16[8,256]{1,0:T(8,128)(2,1)S(1)} %bitcast.4), channel_id=1, source_target_pairs={{0,4},{1,5},{2,6},{3,7},{4,0},{5,1},{6,2},{7,3},{8,12},{9,13},{10,... | collective-permute-start | bytes 12296 | tf_op jit(solution)/shard_map/ppermute | solution.py:438
  65.6 11.6 %collective-permute-start.6 = (bf16[192,256]{1,0:T(8,128)(2,1)S(1)}, bf16[192,256]{1,0:T(8,128)(2,1)S(1)}, u32[]{:S(2)}, u32[]{:S(2)}) collective-permute-start(bf16[192,256]{1,0:T(8,128)(2,1)S(1)} %select_select_fusion.1), channel_id=1, source_target_pairs={{0,6},{8,14},{16,22},{24,30},{32,38},{40,46},{48,54},{56,62},{64,7... | collective-permute-start | bytes 294920 | tf_op jit(solution)/shard_map/ppermute | solution.py:441
  70.0 7.2 %collective-permute-start.5 = (bf16[192,256]{1,0:T(8,128)(2,1)S(1)}, bf16[192,256]{1,0:T(8,128)(2,1)S(1)}, u32[]{:S(2)}, u32[]{:S(2)}) collective-permute-start(bf16[192,256]{1,0:T(8,128)(2,1)S(1)} %select_select_fusion.1), channel_id=1, source_target_pairs={{0,4},{8,12},{16,20},{24,28},{32,36},{40,44},{48,52},{56,60},{64,6... | collective-permute-start | bytes 294920 | tf_op jit(solution)/shard_map/ppermute | solution.py:441
  73.9 3.7 %collective-permute-start.4 = (bf16[192,256]{1,0:T(8,128)(2,1)S(1)}, bf16[192,256]{1,0:T(8,128)(2,1)S(1)}, u32[]{:S(2)}, u32[]{:S(2)}) collective-permute-start(bf16[192,256]{1,0:T(8,128)(2,1)S(1)} %select_select_fusion.1), channel_id=1, source_target_pairs={{0,2},{8,10},{16,18},{24,26},{32,34},{40,42},{48,50},{56,58},{64,6... | collective-permute-start | bytes 294920 | tf_op jit(solution)/shard_map/ppermute | solution.py:441
  75.2 6.4 %collective-permute-start.8 = (bf16[16,256]{1,0:T(8,128)(2,1)S(1)}, bf16[16,256]{1,0:T(8,128)(2,1)S(1)}, u32[]{:S(2)}, u32[]{:S(2)}) collective-permute-start(bf16[16,256]{1,0:T(8,128)(2,1)S(1)} %pad_maximum_fusion.2), channel_id=1, source_target_pairs={{0,2},{1,3},{2,0},{3,1},{4,6},{5,7},{6,4},{7,5},{8,10},{9,11},{10,... | collective-permute-start | bytes 24584 | tf_op jit(solution)/shard_map/ppermute | solution.py:438
  81.7 6.7 %collective-permute-start.9 = (bf16[224,256]{1,0:T(8,128)(2,1)S(1)}, bf16[224,256]{1,0:T(8,128)(2,1)S(1)}, u32[]{:S(2)}, u32[]{:S(2)}) collective-permute-start(bf16[224,256]{1,0:T(8,128)(2,1)S(1)} %pad_maximum_fusion), channel_id=1, source_target_pairs={{0,1},{1,0},{2,3},{3,2},{4,5},{5,4},{6,7},{7,6},{8,9},{9,8},{10,11... | collective-permute-start | bytes 344072 | tf_op jit(solution)/shard_map/ppermute | solution.py:444
  89.2 11.5 %all-to-all-start.2 = ((bf16[4,256,256]{2,1,0:T(8,128)(2,1)}), bf16[4,256,256]{2,1,0:T(8,128)(2,1)S(1)}, u32[]{:S(2)}, u32[]{:S(2)}) async-start(bf16[4,256,256]{2,1,0:T(8,128)(2,1)} %fan_kernel.1), calls=%async_computation.2 | async-start | bytes 1048576 | tf_op jit(solution)/shard_map/all_to_all | solution.py:446
